TPU v7x, 32 devices: a whole 2x2x4 slice. The times are simulated.
32 devices in a mesh: section: 2 (over x), dp: 16 (over z, y, core).
Axes of the slice: x: 2, y: 2, z: 4, core: 2. Of those that a mesh axis runs over, the one named last changes fastest.
Arguments:
- features: bfloat16 [1, 2, 2048, 4096], P(None, 'section', 'dp'), parts along dimension 2, may hold values from -6 to 6
- in_proj: bfloat16 [2, 4096, 512], P('section'), may hold values from -0.09375 to 0.09375
- mix_proj: bfloat16 [2, 2, 256, 256], P('section'), may hold values from -0.375 to 0.375
- out_proj: bfloat16 [2, 512, 4096], P('section'), may hold values from -0.375 to 0.375
- gate_proj: bfloat16 [2, 2, 4096], P('section'), may hold values from -0.09375 to 0.09375
- cross_bias: float32 [2, 4096], P('section'), may hold values from -3 to 3
Outputs:
- crossed: bfloat16 [1, 2, 2048, 4096], P(None, 'section', 'dp'), parts along dimension 2
There are 16 independent parts, one for each index of `dp`. A program takes and returns all parts, laid end to end along the dimension named above; an argument that names none is the same for every part. Nothing has to cross between parts.
All inputs are finite; a program needn't handle non-finite values.
Results may differ from a plain program's by a relative error of at most 0.015.
Values may be sent and summed in bfloat16 or wider, within the bound.
A program may use at most 64 MiB of HBM per device.

v0:
```python
import jax
import jax.numpy as jnp
from jax import lax
from jax.sharding import PartitionSpec as P


def from_behind(block, axis, distance):
    devices = range(lax.axis_size(axis))
    route = [(i - distance, i) for i in devices if i - distance in devices]
    return lax.ppermute(block, axis, route)


def cross_layer(current, anchor, v_mat, c_mat, u_mat, gate_mat, shift_row):
    row_count = current.shape[0]
    expert_count = c_mat.shape[0]
    rank_size = c_mat.shape[1]
    projected = jnp.dot(current, v_mat, preferred_element_type=jnp.float32)
    inner_first = (
        jnp.tanh(projected).astype(jnp.bfloat16).reshape(row_count, expert_count, rank_size)
    )
    inner_second = jnp.einsum(
        "rek,ekj->rej", inner_first, c_mat, preferred_element_type=jnp.float32
    )
    logits = lax.dot_general(
        current, gate_mat, (((1,), (1,)), ((), ())), preferred_element_type=jnp.float32
    )
    gate_values = 1.0 / jnp.sum(jnp.exp(logits[:, None, :] - logits[:, :, None]), axis=2)
    blended = (gate_values[:, :, None] * jnp.tanh(inner_second)).astype(jnp.bfloat16)
    blended = blended.reshape(row_count, expert_count * rank_size)
    crossed = jnp.dot(blended, u_mat, preferred_element_type=jnp.float32)
    updated = current.astype(jnp.float32) + anchor.astype(jnp.float32) * (crossed + shift_row)
    return updated.astype(jnp.bfloat16)


def per_device(features, in_proj, mix_proj, out_proj, gate_proj, cross_bias):
    section_count = lax.axis_size("section")
    position = lax.axis_index("section")
    pieces = 1
    local_micro = features.shape[0]
    row_count = features.shape[2]
    feature_count = features.shape[3]
    piece_rows = row_count // pieces
    everyone = lax.all_gather(features, "section", axis=1, tiled=True)
    all_units = everyone.reshape(local_micro * section_count * pieces, piece_rows, feature_count)
    unit_count = all_units.shape[0]
    step_count = unit_count + section_count - 1
    v_mat = in_proj[0]
    c_mat = mix_proj[0]
    u_mat = out_proj[0]
    gate_mat = gate_proj[0]
    shift_row = cross_bias[0]

    def apply_layer(current, anchor):
        return cross_layer(current, anchor, v_mat, c_mat, u_mat, gate_mat, shift_row)

    def keep_input(current, anchor):
        return current

    def advance(carried, moment):
        incoming, outgoing, collected = carried
        unit_here = moment - position
        active = (unit_here >= 0) & (unit_here < unit_count)
        anchor = lax.dynamic_index_in_dim(
            all_units, jnp.clip(unit_here, 0, unit_count - 1), 0, keepdims=False
        )
        current = jnp.where(position == 0, anchor, incoming)
        result = lax.cond(active, apply_layer, keep_input, current, anchor)
        outgoing = jnp.where(position == section_count - 1, result, outgoing)
        held_unit = moment + position - 2 * section_count + 2
        arrived = (
            (held_unit >= 0)
            & (held_unit < unit_count)
            & (held_unit // pieces % section_count == position)
        )
        held_safe = jnp.clip(held_unit, 0, unit_count - 1)
        slot_index = held_safe // pieces // section_count * pieces + held_safe % pieces
        previous = lax.dynamic_index_in_dim(collected, slot_index, 0, keepdims=False)
        collected = lax.dynamic_update_index_in_dim(
            collected, jnp.where(arrived, outgoing, previous), slot_index, 0
        )
        return (result, outgoing, collected)

    def forward_step(carried, moment):
        result, outgoing, collected = advance(carried, moment)
        incoming = from_behind(result, "section", 1)
        return ((incoming, outgoing, collected), None)

    def cycle_step(carried, moment):
        moved, _ = forward_step(carried, moment)
        incoming, outgoing, collected = moved
        outgoing = from_behind(outgoing, "section", -1)
        return ((incoming, outgoing, collected), None)

    blank = jnp.zeros((piece_rows, feature_count), jnp.bfloat16)
    holding = jnp.zeros((local_micro * pieces, piece_rows, feature_count), jnp.bfloat16)
    carried, _ = lax.scan(
        forward_step, (blank, blank, holding), jnp.arange(0, section_count - 1, dtype=jnp.int32)
    )
    carried, _ = lax.scan(
        cycle_step, carried, jnp.arange(section_count - 1, step_count - 1, dtype=jnp.int32)
    )
    _, _, collected = advance(carried, jnp.int32(step_count - 1))
    return collected.reshape(local_micro, 1, row_count, feature_count)


def solution(mesh):
    placed = (
        P(None, "section", "dp", None),
        P("section", None, None),
        P("section", None, None, None),
        P("section", None, None),
        P("section", None, None),
        P("section", None),
    )
    return jax.shard_map(
        per_device,
        mesh=mesh,
        in_specs=placed,
        out_specs=P(None, "section", "dp", None),
        check_vma=False,
    )
```

profile of v0, /device:TPU:2, one launch (start us, length us, event | category | flops | bytes accessed | tf_op | source)
XLA Modules:
  0.0 130.4 jit_solution(13214571090702250396)
XLA Ops:
  6.5 0.0 all-gather.2.cloned.1.call-start
  6.5 0.7 all-gather.2.cloned.1.call-update
  7.3 34.8 %all-gather.2.cloned.1.call-done = bf16[1,2,128,4096]{3,2,0,1:T(8,128)(2,1)} async-done(((bf16[1,1,128,4096]{3,2,0,1:T(8,128)(2,1)}), bf16[1,2,128,4096]{3,2,0,1:T(8,128)(2,1)}) %all-gather.2.cloned.1.call-update) | async-done | bytes 2097168 | tf_op jit(solution)/shard_map/all_gather | solution.py:43
  42.1 1.4 %broadcast_select_fusion.2 = (bf16[128,4096]{1,0:T(8,128)(2,1)S(1)}, bf16[128,4096]{1,0:T(8,128)(2,1)S(1)}) fusion(pred[]{:T(512)S(6)} %eq.38, bf16[1,2,128,4096]{3,2,0,1:T(8,128)(2,1)} %all-gather.2.cloned.1.call-done, s32[]{:T(128)S(6)} %min.19), kind=kLoop, calls=%fused_computation.48 | loop fusion | flops 524288 | bytes 3145733 | tf_op jit(solution)/shard_map/while/body/eval_jaxpr/jit(_where)/select_n | solution.py:66
  43.5 0.0 copy-done
  43.5 0.0 copy-done.1
  43.5 0.0 copy-done.2
  43.5 1.3 collective-permute-start
  44.8 32.0 %collective-permute-done = bf16[128,4096]{1,0:T(8,128)(2,1)} collective-permute-done((bf16[128,4096]{1,0:T(8,128)(2,1)S(1)}, bf16[128,4096]{1,0:T(8,128)(2,1)}, u32[]{:S(2)}, u32[]{:S(2)}) %collective-permute-start) | collective-permute-done | bytes 1048608 | tf_op jit(solution)/shard_map/while/body/eval_jaxpr/ppermute | solution.py:10
  76.8 1.7 %broadcast_select_fusion.1 = (bf16[128,4096]{1,0:T(8,128)(2,1)S(1)}, bf16[128,4096]{1,0:T(8,128)(2,1)S(1)}) fusion(bf16[128,4096]{1,0:T(8,128)(2,1)} %collective-permute-done, pred[]{:T(512)S(6)} %eq.38, bf16[1,2,128,4096]{3,2,0,1:T(8,128)(2,1)} %all-gather.2.cloned.1.call-done, s32[]{:T(128)S(6)} %min.18), kind=kLoop, calls=%fused_computation.47 | loop fusion | flops 524288 | bytes 4194309 | tf_op jit(solution)/shard_map/while/body/eval_jaxpr/jit(_where)/select_n | solution.py:66
  78.5 7.3 %conditional.4 = (bf16[128,4096]{1,0:T(8,128)(2,1)S(1)}) conditional(s32[]{:T(128)} %convert_element_type.57, bf16[128,4096]{1,0:T(8,128)(2,1)S(1)} %get-tuple-element.150, (bf16[128,4096]{1,0:T(8,128)(2,1)S(1)}, bf16[128,4096]{1,0:T(8,128)(2,1)S(1)}, bf16[2,4096]{1,0:T(2,128)(2,1)S(1)}, bf16[4096,512]{1,0:T(8,128)(2,1)}, ...), branch_computations={%region_3.4_spmd, %region_4.6_spmd} | conditional | flops 1112736768 | bytes 15767588 | solution.py:67
  78.5 0.0 copy-start.3
  78.5 3.0 %fusion.14 = bf16[128,512]{1,0:T(8,128)(2,1)S(1)} fusion(bf16[128,4096]{1,0:T(8,128)(2,1)S(1)} %get-tuple-element.134, bf16[4096,512]{1,0:T(8,128)(2,1)} %get-tuple-element.137), kind=kOutput, calls=%fused_computation.22 | convolution fusion | flops 536936448 | bytes 5373952 | tf_op jit(solution)/shard_map/while/body/eval_jaxpr/cond/branch_1_fun/dot_general | solution.py:17
  81.5 0.4 fusion.28
  81.9 0.0 copy-done.3
  82.0 0.2 fusion.15
  82.2 0.1 copy.44
  82.3 3.6 %fusion.11 = bf16[128,4096]{1,0:T(8,128)(2,1)S(1)} fusion(bf16[128,512]{0,1:T(8,128)(2,1)S(1)} %bitcast.81, bf16[512,4096]{1,0:T(8,128)(2,1)} %get-tuple-element.139, bf16[128,4096]{1,0:T(8,128)(2,1)S(1)} %get-tuple-element.135, bf16[128,4096]{1,0:T(8,128)(2,1)S(1)} %get-tuple-element.134, f32[4096]{0:T(1024)S(1)} %bitcast.87), kind=kOutput, calls=%fused_computation.17 | convolution fusion | flops 540016640 | bytes 7487488 | tf_op jit(solution)/shard_map/while/body/eval_jaxpr/cond/branch_1_fun/dot_general | solution.py:30
  85.9 1.3 collective-permute-start.1
  87.2 1.1 broadcast_select_fusion.3
  88.3 6.5 %collective-permute-start.2 = (bf16[128,4096]{1,0:T(8,128)(2,1)}, bf16[128,4096]{1,0:T(8,128)(2,1)}, u32[]{:S(2)}, u32[]{:S(2)}) collective-permute-start(bf16[128,4096]{1,0:T(8,128)(2,1)} %broadcast_select_fusion.3), channel_id=1, source_target_pairs={{16,0},{17,1},{18,2},{19,3},{20,4},{21,5},{22,6},{23,7},{24,8},{25... | collective-permute-start | bytes 3145736 | tf_op jit(solution)/shard_map/while/body/eval_jaxpr/ppermute | solution.py:10
  94.8 17.2 %collective-permute-done.1 = bf16[128,4096]{1,0:T(8,128)(2,1)} collective-permute-done((bf16[128,4096]{1,0:T(8,128)(2,1)S(1)}, bf16[128,4096]{1,0:T(8,128)(2,1)}, u32[]{:S(2)}, u32[]{:S(2)}) %collective-permute-start.1) | collective-permute-done | bytes 1048608 | tf_op jit(solution)/shard_map/while/body/eval_jaxpr/ppermute | solution.py:10
  112.0 2.6 %broadcast_select_fusion = (bf16[128,4096]{1,0:T(8,128)(2,1)S(1)}, bf16[128,4096]{1,0:T(8,128)(2,1)}) fusion(bf16[128,4096]{1,0:T(8,128)(2,1)} %collective-permute-done.1, pred[]{:T(512)S(6)} %eq.38, bf16[1,2,128,4096]{3,2,0,1:T(8,128)(2,1)} %all-gather.2.cloned.1.call-done, s32[]{:T(128)S(6)} %min.17), kind=kLoop, calls=%fused_computation.46 | loop fusion | flops 524288 | bytes 4194309 | tf_op jit(solution)/shard_map/jit(_where)/select_n | solution.py:66
  114.7 7.6 %conditional.5 = (bf16[128,4096]{1,0:T(8,128)(2,1)S(1)}) conditional(s32[]{:T(128)} %convert_element_type.56, bf16[128,4096]{1,0:T(8,128)(2,1)S(1)} %get-tuple-element.148, (bf16[128,4096]{1,0:T(8,128)(2,1)S(1)}, bf16[128,4096]{1,0:T(8,128)(2,1)}, bf16[2,4096]{1,0:T(2,128)(2,1)S(1)}, bf16[4096,512]{1,0:T(8,128)(2,1)}, bf16[2,256,256]{2,1,0:T(8,128)(2,1)}, ...), branch_computations={%region_6.7_spmd, %region_7.9_spmd} | conditional | flops 1112736768 | bytes 15767588 | solution.py:67
  114.7 3.0 %fusion.23 = bf16[128,512]{1,0:T(8,128)(2,1)S(1)} fusion(bf16[128,4096]{1,0:T(8,128)(2,1)S(1)} %get-tuple-element.141, bf16[4096,512]{1,0:T(8,128)(2,1)} %get-tuple-element.144), kind=kOutput, calls=%fused_computation.36 | convolution fusion | flops 536936448 | bytes 5373952 | tf_op jit(solution)/shard_map/cond/branch_1_fun/dot_general | solution.py:17
  117.7 0.4 fusion.29
  118.1 0.0 copy-done.4
  118.1 0.2 fusion.24
  118.3 0.1 copy.46
  118.4 3.9 %fusion.20 = bf16[128,4096]{1,0:T(8,128)(2,1)S(1)} fusion(bf16[128,512]{0,1:T(8,128)(2,1)S(1)} %bitcast.82, bf16[512,4096]{1,0:T(8,128)(2,1)} %get-tuple-element.146, bf16[128,4096]{1,0:T(8,128)(2,1)} %get-tuple-element.142, bf16[128,4096]{1,0:T(8,128)(2,1)S(1)} %get-tuple-element.141, f32[4096]{0:T(1024)S(1)} %bitcast.88), kind=kOutput, calls=%fused_computation.31 | convolution fusion | flops 540016640 | bytes 7487488 | tf_op jit(solution)/shard_map/cond/branch_1_fun/dot_general | solution.py:30
  122.3 0.0 collective-permute-done.2
  122.3 1.2 select_bitcast_fusion
  (9 shorter events, 0.1 us)
Async XLA Ops:
  6.5 35.6 %all-gather.2.cloned.1.call-start = ((), (), s32[]{:S(2)}) async-start(), calls=%async_computation | async-start | bytes 3145728 | tf_op jit(solution)/shard_map/all_gather | solution.py:43
  6.5 36.9 %copy-start = (bf16[1,2,4096]{2,1,0:T(2,128)(2,1)S(1)}, bf16[1,2,4096]{2,1,0:T(2,128)(2,1)}, u32[]{:S(2)}) copy-start(bf16[1,2,4096]{2,1,0:T(2,128)(2,1)} %param.16) | copy-start | bytes 49156
  6.5 36.9 %copy-start.1 = (f32[1,4096]{1,0:T(1,128)S(1)}, f32[1,4096]{1,0:T(1,128)}, u32[]{:S(2)}) copy-start(f32[1,4096]{1,0:T(1,128)} %param.17) | copy-start | bytes 49156
  6.5 36.9 %copy-start.2 = (bf16[1,2,256,256]{3,2,1,0:T(8,128)(2,1)S(1)}, bf16[1,2,256,256]{3,2,1,0:T(8,128)(2,1)}, u32[]{:S(2)}) copy-start(bf16[1,2,256,256]{3,2,1,0:T(8,128)(2,1)} %param.14) | copy-start | bytes 786436
  43.5 33.3 %collective-permute-start = (bf16[128,4096]{1,0:T(8,128)(2,1)S(1)}, bf16[128,4096]{1,0:T(8,128)(2,1)}, u32[]{:S(2)}, u32[]{:S(2)}) collective-permute-start(bf16[128,4096]{1,0:T(8,128)(2,1)S(1)} %get-tuple-element.154), channel_id=1, source_target_pairs={{0,16},{1,17},{2,18},{3,19},{4,20},{5,21},{6,22},{7,23},{8,24},{9,... | collective-permute-start | bytes 3145736 | tf_op jit(solution)/shard_map/while/body/eval_jaxpr/ppermute | solution.py:10
  78.5 3.4 %copy-start.3 = (bf16[2,256,256]{2,1,0:T(8,128)(2,1)S(1)}, bf16[2,256,256]{2,1,0:T(8,128)(2,1)}, u32[]{:S(2)}) copy-start(bf16[2,256,256]{2,1,0:T(8,128)(2,1)} %get-tuple-element.138) | copy-start | bytes 786436 | tf_op jit(solution)/shard_map/while/body/eval_jaxpr/cond
  85.9 26.2 %collective-permute-start.1 = (bf16[128,4096]{1,0:T(8,128)(2,1)S(1)}, bf16[128,4096]{1,0:T(8,128)(2,1)}, u32[]{:S(2)}, u32[]{:S(2)}) collective-permute-start(bf16[128,4096]{1,0:T(8,128)(2,1)S(1)} %get-tuple-element.155), channel_id=1, source_target_pairs={{0,16},{1,17},{2,18},{3,19},{4,20},{5,21},{6,22},{7,23},{8,24},{9,... | collective-permute-start | bytes 3145736 | tf_op jit(solution)/shard_map/while/body/eval_jaxpr/ppermute | solution.py:10
  88.3 34.0 %collective-permute-start.2 = (bf16[128,4096]{1,0:T(8,128)(2,1)}, bf16[128,4096]{1,0:T(8,128)(2,1)}, u32[]{:S(2)}, u32[]{:S(2)}) collective-permute-start(bf16[128,4096]{1,0:T(8,128)(2,1)} %broadcast_select_fusion.3), channel_id=1, source_target_pairs={{16,0},{17,1},{18,2},{19,3},{20,4},{21,5},{22,6},{23,7},{24,8},{25... | collective-permute-start | bytes 3145736 | tf_op jit(solution)/shard_map/while/body/eval_jaxpr/ppermute | solution.py:10
  114.7 3.4 %copy-start.4 = (bf16[2,256,256]{2,1,0:T(8,128)(2,1)S(1)}, bf16[2,256,256]{2,1,0:T(8,128)(2,1)}, u32[]{:S(2)}) copy-start(bf16[2,256,256]{2,1,0:T(8,128)(2,1)} %get-tuple-element.145) | copy-start | bytes 786436 | tf_op jit(solution)/shard_map/cond
Sparse Core Ops, SparseCore 0:
  8.9 33.1 all-gather.1
where the time goes:
time: 131 us; the launch traced here: 130 us
  waiting for transfers between devices  84.8 us (65%)
  matrix products  14.5 us (11%)
  between operations  13.5 us (10%)
  starting transfers between devices  9.1 us (7%)
  other arithmetic  8.06 us (6%)
    ppermute x3, waiting for transfers between devices, from_behind(): return lax.ppermute(block, axis, route)  49.3 us
    all_gather x1, waiting for transfers between devices, per_device(): everyone = lax.all_gather(features, 'section', axis=1, tiled=True)  34.8 us
    ppermute x3, starting transfers between devices, from_behind(): return lax.ppermute(block, axis, route)  9.1 us
    dot_general x2, matrix products, cross_layer(): crossed = jnp.dot(blended, u_mat, preferred_element_type=jnp.float32)  7.47 us
    dot_general x2, matrix products, cross_layer(): projected = jnp.dot(current, v_mat, preferred_element_type=jnp.float32)  5.91 us
    select_n x3, other arithmetic, advance(): current = jnp.where(position == 0, anchor, incoming)  5.69 us
  transfers between devices with their start and end apart: 4, of which 3 were waited for; matrix products, arithmetic and copies ran while one was open for 9% of the time, Pallas kernels for 0%

commit v1 on v0

--- a/solution.py
+++ b/solution.py
@@ -2,6 +2,7 @@
 import jax.numpy as jnp
 from jax import lax
 from jax.sharding import PartitionSpec as P
+from jax.lax import all_gather
 
 
 def from_behind(block, axis, distance):
@@ -40,7 +41,7 @@
     row_count = features.shape[2]
     feature_count = features.shape[3]
     piece_rows = row_count // pieces
-    everyone = lax.all_gather(features, "section", axis=1, tiled=True)
+    everyone = jnp.concatenate(all_gather(features, "section"), axis=1)
     all_units = everyone.reshape(local_micro * section_count * pieces, piece_rows, feature_count)
     unit_count = all_units.shape[0]
     step_count = unit_count + section_count - 1

time: 131 us -> 131 us (level)
  no operation moved by 1% of the time
where the time goes in v1:
time: 131 us; the launch traced here: 130 us
  waiting for transfers between devices  84.8 us (65%)
  matrix products  14.5 us (11%)
  between operations  13.5 us (10%)
  starting transfers between devices  9.1 us (7%)
  other arithmetic  8.06 us (6%)
    ppermute x3, waiting for transfers between devices, from_behind(): return lax.ppermute(block, axis, route)  49.3 us
    all_gather x1, waiting for transfers between devices, per_device(): everyone = jnp.concatenate(all_gather(features, 'section'), axis=1)  34.8 us
    ppermute x3, starting transfers between devices, from_behind(): return lax.ppermute(block, axis, route)  9.1 us
    dot_general x2, matrix products, cross_layer(): crossed = jnp.dot(blended, u_mat, preferred_element_type=jnp.float32)  7.47 us
    dot_general x2, matrix products, cross_layer(): projected = jnp.dot(current, v_mat, preferred_element_type=jnp.float32)  5.91 us
    select_n x3, other arithmetic, advance(): current = jnp.where(position == 0, anchor, incoming)  5.69 us
  transfers between devices with their start and end apart: 4, of which 3 were waited for; matrix products, arithmetic and copies ran while one was open for 9% of the time, Pallas kernels for 0%

profile of v1, /device:TPU:2, one launch (start us, length us, event | category | flops | bytes accessed | tf_op | source)
XLA Modules:
  0.0 130.4 jit_solution(2403684734066788996)
XLA Ops:
  6.5 0.0 all-gather.3.cloned.1.call-start
  6.5 0.7 all-gather.3.cloned.1.call-update
  7.3 34.8 %all-gather.3.cloned.1.call-done = bf16[2,1,128,4096]{3,2,1,0:T(8,128)(2,1)} async-done(((bf16[1,1,128,4096]{3,2,1,0:T(8,128)(2,1)}), bf16[2,1,128,4096]{3,2,1,0:T(8,128)(2,1)}) %all-gather.3.cloned.1.call-update) | async-done | bytes 2097168 | tf_op jit(solution)/shard_map/all_gather | solution.py:44
  42.1 1.4 %broadcast_select_fusion.2 = (bf16[128,4096]{1,0:T(8,128)(2,1)S(1)}, bf16[128,4096]{1,0:T(8,128)(2,1)S(1)}) fusion(pred[]{:T(512)S(6)} %eq.38, bf16[2,1,128,4096]{3,2,1,0:T(8,128)(2,1)} %all-gather.3.cloned.1.call-done, s32[]{:T(128)S(6)} %min.19), kind=kLoop, calls=%fused_computation.48 | loop fusion | flops 524288 | bytes 3145733 | tf_op jit(solution)/shard_map/while/body/eval_jaxpr/jit(_where)/select_n | solution.py:67
  43.5 0.0 copy-done
  43.5 0.0 copy-done.2
  43.5 0.0 copy-done.1
  43.5 1.3 collective-permute-start
  44.8 32.0 %collective-permute-done = bf16[128,4096]{1,0:T(8,128)(2,1)} collective-permute-done((bf16[128,4096]{1,0:T(8,128)(2,1)S(1)}, bf16[128,4096]{1,0:T(8,128)(2,1)}, u32[]{:S(2)}, u32[]{:S(2)}) %collective-permute-start) | collective-permute-done | bytes 1048608 | tf_op jit(solution)/shard_map/while/body/eval_jaxpr/ppermute | solution.py:11
  76.9 1.7 %broadcast_select_fusion.1 = (bf16[128,4096]{1,0:T(8,128)(2,1)S(1)}, bf16[128,4096]{1,0:T(8,128)(2,1)S(1)}) fusion(bf16[128,4096]{1,0:T(8,128)(2,1)} %collective-permute-done, pred[]{:T(512)S(6)} %eq.38, bf16[2,1,128,4096]{3,2,1,0:T(8,128)(2,1)} %all-gather.3.cloned.1.call-done, s32[]{:T(128)S(6)} %min.18), kind=kLoop, calls=%fused_computation.47 | loop fusion | flops 524288 | bytes 4194309 | tf_op jit(solution)/shard_map/while/body/eval_jaxpr/jit(_where)/select_n | solution.py:67
  78.5 7.3 %conditional.4 = (bf16[128,4096]{1,0:T(8,128)(2,1)S(1)}) conditional(s32[]{:T(128)} %convert_element_type.57, bf16[128,4096]{1,0:T(8,128)(2,1)S(1)} %get-tuple-element.150, (bf16[128,4096]{1,0:T(8,128)(2,1)S(1)}, bf16[128,4096]{1,0:T(8,128)(2,1)S(1)}, bf16[2,4096]{1,0:T(2,128)(2,1)S(1)}, bf16[4096,512]{1,0:T(8,128)(2,1)}, ...), branch_computations={%region_3.4_spmd, %region_4.6_spmd} | conditional | flops 1112736768 | bytes 15767588 | solution.py:68
  78.5 0.0 copy-start.3
  78.6 3.0 %fusion.14 = bf16[128,512]{1,0:T(8,128)(2,1)S(1)} fusion(bf16[128,4096]{1,0:T(8,128)(2,1)S(1)} %get-tuple-element.134, bf16[4096,512]{1,0:T(8,128)(2,1)} %get-tuple-element.137), kind=kOutput, calls=%fused_computation.22 | convolution fusion | flops 536936448 | bytes 5373952 | tf_op jit(solution)/shard_map/while/body/eval_jaxpr/cond/branch_1_fun/dot_general | solution.py:18
  81.5 0.4 fusion.28
  82.0 0.0 copy-done.3
  82.0 0.2 fusion.15
  82.2 0.1 copy.43
  82.3 3.6 %fusion.11 = bf16[128,4096]{1,0:T(8,128)(2,1)S(1)} fusion(bf16[128,512]{0,1:T(8,128)(2,1)S(1)} %bitcast.79, bf16[512,4096]{1,0:T(8,128)(2,1)} %get-tuple-element.139, bf16[128,4096]{1,0:T(8,128)(2,1)S(1)} %get-tuple-element.135, bf16[128,4096]{1,0:T(8,128)(2,1)S(1)} %get-tuple-element.134, f32[4096]{0:T(1024)S(1)} %bitcast.85), kind=kOutput, calls=%fused_computation.17 | convolution fusion | flops 540016640 | bytes 7487488 | tf_op jit(solution)/shard_map/while/body/eval_jaxpr/cond/branch_1_fun/dot_general | solution.py:31
  85.9 1.3 collective-permute-start.1
  87.2 1.1 broadcast_select_fusion.3
  88.3 6.5 %collective-permute-start.2 = (bf16[128,4096]{1,0:T(8,128)(2,1)}, bf16[128,4096]{1,0:T(8,128)(2,1)}, u32[]{:S(2)}, u32[]{:S(2)}) collective-permute-start(bf16[128,4096]{1,0:T(8,128)(2,1)} %broadcast_select_fusion.3), channel_id=1, source_target_pairs={{16,0},{17,1},{18,2},{19,3},{20,4},{21,5},{22,6},{23,7},{24,8},{25... | collective-permute-start | bytes 3145736 | tf_op jit(solution)/shard_map/while/body/eval_jaxpr/ppermute | solution.py:11
  94.8 17.2 %collective-permute-done.1 = bf16[128,4096]{1,0:T(8,128)(2,1)} collective-permute-done((bf16[128,4096]{1,0:T(8,128)(2,1)S(1)}, bf16[128,4096]{1,0:T(8,128)(2,1)}, u32[]{:S(2)}, u32[]{:S(2)}) %collective-permute-start.1) | collective-permute-done | bytes 1048608 | tf_op jit(solution)/shard_map/while/body/eval_jaxpr/ppermute | solution.py:11
  112.0 2.6 %broadcast_select_fusion = (bf16[128,4096]{1,0:T(8,128)(2,1)S(1)}, bf16[128,4096]{1,0:T(8,128)(2,1)}) fusion(bf16[128,4096]{1,0:T(8,128)(2,1)} %collective-permute-done.1, pred[]{:T(512)S(6)} %eq.38, bf16[2,1,128,4096]{3,2,1,0:T(8,128)(2,1)} %all-gather.3.cloned.1.call-done, s32[]{:T(128)S(6)} %min.17), kind=kLoop, calls=%fused_computation.46 | loop fusion | flops 524288 | bytes 4194309 | tf_op jit(solution)/shard_map/jit(_where)/select_n | solution.py:67
  114.7 7.6 %conditional.5 = (bf16[128,4096]{1,0:T(8,128)(2,1)S(1)}) conditional(s32[]{:T(128)} %convert_element_type.56, bf16[128,4096]{1,0:T(8,128)(2,1)S(1)} %get-tuple-element.148, (bf16[128,4096]{1,0:T(8,128)(2,1)S(1)}, bf16[128,4096]{1,0:T(8,128)(2,1)}, bf16[2,4096]{1,0:T(2,128)(2,1)S(1)}, bf16[4096,512]{1,0:T(8,128)(2,1)}, bf16[2,256,256]{2,1,0:T(8,128)(2,1)}, ...), branch_computations={%region_6.7_spmd, %region_7.9_spmd} | conditional | flops 1112736768 | bytes 15767588 | solution.py:68
  114.7 3.0 %fusion.23 = bf16[128,512]{1,0:T(8,128)(2,1)S(1)} fusion(bf16[128,4096]{1,0:T(8,128)(2,1)S(1)} %get-tuple-element.141, bf16[4096,512]{1,0:T(8,128)(2,1)} %get-tuple-element.144), kind=kOutput, calls=%fused_computation.36 | convolution fusion | flops 536936448 | bytes 5373952 | tf_op jit(solution)/shard_map/cond/branch_1_fun/dot_general | solution.py:18
  117.7 0.4 fusion.29
  118.1 0.0 copy-done.4
  118.1 0.2 fusion.24
  118.3 0.1 copy.45
  118.4 3.9 %fusion.20 = bf16[128,4096]{1,0:T(8,128)(2,1)S(1)} fusion(bf16[128,512]{0,1:T(8,128)(2,1)S(1)} %bitcast.80, bf16[512,4096]{1,0:T(8,128)(2,1)} %get-tuple-element.146, bf16[128,4096]{1,0:T(8,128)(2,1)} %get-tuple-element.142, bf16[128,4096]{1,0:T(8,128)(2,1)S(1)} %get-tuple-element.141, f32[4096]{0:T(1024)S(1)} %bitcast.86), kind=kOutput, calls=%fused_computation.31 | convolution fusion | flops 540016640 | bytes 7487488 | tf_op jit(solution)/shard_map/cond/branch_1_fun/dot_general | solution.py:31
  122.3 0.0 collective-permute-done.2
  122.3 1.2 select_bitcast_fusion
  (9 shorter events, 0.1 us)
Async XLA Ops:
  6.5 36.9 %copy-start = (bf16[1,2,4096]{2,1,0:T(2,128)(2,1)S(1)}, bf16[1,2,4096]{2,1,0:T(2,128)(2,1)}, u32[]{:S(2)}) copy-start(bf16[1,2,4096]{2,1,0:T(2,128)(2,1)} %param.16) | copy-start | bytes 49156
  6.5 36.9 %copy-start.2 = (bf16[1,2,256,256]{3,2,1,0:T(8,128)(2,1)S(1)}, bf16[1,2,256,256]{3,2,1,0:T(8,128)(2,1)}, u32[]{:S(2)}) copy-start(bf16[1,2,256,256]{3,2,1,0:T(8,128)(2,1)} %param.14) | copy-start | bytes 786436
  6.5 37.0 %copy-start.1 = (f32[1,4096]{1,0:T(1,128)S(1)}, f32[1,4096]{1,0:T(1,128)}, u32[]{:S(2)}) copy-start(f32[1,4096]{1,0:T(1,128)} %param.17) | copy-start | bytes 49156
  6.5 35.6 %all-gather.3.cloned.1.call-start = ((), (), s32[]{:S(2)}) async-start(), calls=%async_computation | async-start | bytes 3145728 | tf_op jit(solution)/shard_map/all_gather | solution.py:44
  43.5 33.3 %collective-permute-start = (bf16[128,4096]{1,0:T(8,128)(2,1)S(1)}, bf16[128,4096]{1,0:T(8,128)(2,1)}, u32[]{:S(2)}, u32[]{:S(2)}) collective-permute-start(bf16[128,4096]{1,0:T(8,128)(2,1)S(1)} %get-tuple-element.154), channel_id=1, source_target_pairs={{0,16},{1,17},{2,18},{3,19},{4,20},{5,21},{6,22},{7,23},{8,24},{9,... | collective-permute-start | bytes 3145736 | tf_op jit(solution)/shard_map/while/body/eval_jaxpr/ppermute | solution.py:11
  78.5 3.4 %copy-start.3 = (bf16[2,256,256]{2,1,0:T(8,128)(2,1)S(1)}, bf16[2,256,256]{2,1,0:T(8,128)(2,1)}, u32[]{:S(2)}) copy-start(bf16[2,256,256]{2,1,0:T(8,128)(2,1)} %get-tuple-element.138) | copy-start | bytes 786436 | tf_op jit(solution)/shard_map/while/body/eval_jaxpr/cond
  85.9 26.2 %collective-permute-start.1 = (bf16[128,4096]{1,0:T(8,128)(2,1)S(1)}, bf16[128,4096]{1,0:T(8,128)(2,1)}, u32[]{:S(2)}, u32[]{:S(2)}) collective-permute-start(bf16[128,4096]{1,0:T(8,128)(2,1)S(1)} %get-tuple-element.155), channel_id=1, source_target_pairs={{0,16},{1,17},{2,18},{3,19},{4,20},{5,21},{6,22},{7,23},{8,24},{9,... | collective-permute-start | bytes 3145736 | tf_op jit(solution)/shard_map/while/body/eval_jaxpr/ppermute | solution.py:11
  88.3 34.0 %collective-permute-start.2 = (bf16[128,4096]{1,0:T(8,128)(2,1)}, bf16[128,4096]{1,0:T(8,128)(2,1)}, u32[]{:S(2)}, u32[]{:S(2)}) collective-permute-start(bf16[128,4096]{1,0:T(8,128)(2,1)} %broadcast_select_fusion.3), channel_id=1, source_target_pairs={{16,0},{17,1},{18,2},{19,3},{20,4},{21,5},{22,6},{23,7},{24,8},{25... | collective-permute-start | bytes 3145736 | tf_op jit(solution)/shard_map/while/body/eval_jaxpr/ppermute | solution.py:11
  114.7 3.4 %copy-start.4 = (bf16[2,256,256]{2,1,0:T(8,128)(2,1)S(1)}, bf16[2,256,256]{2,1,0:T(8,128)(2,1)}, u32[]{:S(2)}) copy-start(bf16[2,256,256]{2,1,0:T(8,128)(2,1)} %get-tuple-element.145) | copy-start | bytes 786436 | tf_op jit(solution)/shard_map/cond
Sparse Core Ops, SparseCore 0:
  8.9 33.1 all-gather.2
